TPU v7x, 256 devices: a whole 4x4x8 slice. The times are simulated.
256 devices in a mesh: replica: 32 (over y, z), expert: 8 (over x, core).
Axes of the slice: x: 4, y: 4, z: 8, core: 2. Of those that a mesh axis runs over, the one named last changes fastest.
Arguments:
- outer_params: float32 [28672, 4096], P('expert', 'replica'), may hold values from -6 to 6
- momentum: bfloat16 [28672, 4096], P('expert', 'replica'), may hold values from -6 to 6
- replica_deltas: bfloat16 [32, 16, 128, 4096], P('replica', 'expert'), may hold values from -6 to 6
- replica_rows: bfloat16 [32, 16, 128, 4096], P('replica', 'expert'), may hold values from -6 to 6
- block_ids: int32 [32, 16], P('replica', 'expert'), may hold values from 0 to 223, as said below
- slot_counts: int32 [32, 8], P('replica', 'expert'), may hold values from 0 to 2, as said below
Outputs:
- new_params: float32 [28672, 4096], P('expert', 'replica')
- new_momentum: bfloat16 [28672, 4096], P('expert', 'replica')
- blended_rows: bfloat16 [32, 16, 128, 4096], P('replica', 'expert')
Inputs may be any that keep to these rules, and one draw needn't show every extreme that they name: `block_ids`: within row r, slots e * 2 to (e + 1) * 2 - 1 name distinct blocks among e * 28 to (e + 1) * 28 - 1. The first slot_counts[r, e] slots of group e of row r are live, the rest are padding; in every draw some index e has 2 in every row.
All inputs are finite; a program needn't handle non-finite values.
Results may differ from a plain program's by a relative error of at most 0.0075.
Values may be sent and summed in bfloat16 or wider, within the bound.
A program may use at most 64 MiB of HBM per device.

v0:
```python
import jax
import jax.numpy as jnp
from jax import lax
from jax.sharding import PartitionSpec as P

outer_rate = 0.7
nesterov_decay = 0.9
blend_weight = 0.5


def laid_out(tiles, dim):
    tiles = jnp.moveaxis(tiles, 0, dim)
    dims = tiles.shape
    return tiles.reshape(*dims[:dim], dims[dim] * dims[dim + 1], *dims[dim + 2 :])


def gather_packed(arrays, axis, dims):
    ravelled = jnp.concatenate([a.reshape(-1) for a in arrays])
    lines, at, gathered = (lax.all_gather(ravelled, axis), 0, [])
    for a, dim in zip(arrays, dims):
        tiles = lines[:, at : at + a.size].reshape(-1, *a.shape)
        gathered.append(laid_out(tiles, dim))
        at += a.size
    return tuple(gathered)


def local(outer_params, momentum, replica_deltas, replica_rows, block_ids, slot_counts):
    slot_total = block_ids.shape[1]
    block_size = replica_deltas.shape[2]
    width_slab = outer_params.shape[1]
    block_count = outer_params.shape[0] // block_size
    expert_index = lax.axis_index("expert")
    all_ids, all_counts = gather_packed((block_ids, slot_counts), "replica", (0, 0))
    positions = jnp.arange(slot_total, dtype=jnp.int32)
    live_flags = (positions[None, :] < all_counts).reshape(-1)
    local_ids = (all_ids - expert_index * block_count).reshape(-1)
    selector = (
        local_ids[None, :] == jnp.arange(block_count, dtype=jnp.int32)[:, None]
    ) & live_flags[None, :]
    selector_float = selector.astype(jnp.float32)
    tallies = jnp.sum(selector_float, axis=1)
    received = lax.all_to_all(replica_deltas[0], "replica", split_axis=2, concat_axis=0, tiled=True)
    totals = jnp.einsum(
        "bs,sic->bic", selector.astype(jnp.bfloat16), received, preferred_element_type=jnp.float32
    )
    mean_delta = (totals / jnp.maximum(tallies, 1.0)[:, None, None]).reshape(outer_params.shape)
    moment = nesterov_decay * momentum.astype(jnp.float32) + mean_delta
    params_new = outer_params - outer_rate * (mean_delta + nesterov_decay * moment)
    blocks_new = params_new.reshape(block_count, block_size, width_slab)
    fetched = jnp.einsum(
        "bs,bic->sic", selector_float, blocks_new, precision=lax.Precision.HIGHEST
    ).astype(jnp.bfloat16)
    returned = lax.all_to_all(fetched, "replica", split_axis=0, concat_axis=2, tiled=True)
    own_flags = (positions < slot_counts[0, 0])[:, None, None]
    rows_float = replica_rows[0].astype(jnp.float32)
    mixed = blend_weight * rows_float + (1.0 - blend_weight) * returned.astype(jnp.float32)
    blended = jnp.where(own_flags, mixed, rows_float).astype(jnp.bfloat16)
    return (params_new, moment.astype(jnp.bfloat16), blended[None])


def solution(mesh):
    in_specs = (
        P("expert", "replica"),
        P("expert", "replica"),
        P("replica", "expert", None, None),
        P("replica", "expert", None, None),
        P("replica", "expert"),
        P("replica", "expert"),
    )
    out_specs = (P("expert", "replica"), P("expert", "replica"), P("replica", "expert", None, None))
    return jax.shard_map(local, mesh=mesh, in_specs=in_specs, out_specs=out_specs, check_vma=False)
```

profile of v0, /device:TPU:64, one launch (start us, length us, event | category | flops | bytes accessed | tf_op | source)
XLA Modules:
  0.0 163.8 jit_solution(16776409106038687696)
XLA Ops:
  0.6 6.2 %copy.16 = bf16[1,2,128,4096]{2,1,3,0:T(2,128)(2,1)} copy(bf16[1,2,128,4096]{3,2,1,0:T(8,128)(2,1)} %param.8) | data formatting | bytes 4194304 | tf_op args[2]
  6.8 11.0 %all-to-all-start = ((bf16[2,128,4096]{1,0,2:T(2,128)(2,1)}), bf16[2,128,4096]{1,0,2:T(2,128)(2,1)S(1)}, u32[]{:S(2)}, u32[]{:S(2)}) async-start(bf16[2,128,4096]{1,0,2:T(2,128)(2,1)} %bitcast.37), calls=%async_computation | async-start | bytes 4194304 | tf_op jit(solution)/shard_map/all_to_all | solution.py:42
  18.5 0.0 copy-done.5
  18.5 0.6 dynamic-slice
  19.8 0.0 copy-done.4
  19.8 0.2 add_dynamic-update-slice_fusion
  19.9 60.3 %all-reduce = s32[96]{0:T(128)S(1)} all-reduce(s32[96]{0:T(128)S(1)} %add_dynamic-update-slice_fusion), channel_id=2, replica_groups=mesh['replica'=32,'expert'=8] {'replica'}, use_global_device_ids=true, to_apply=%add | all-reduce | flops 96 | bytes 768
  80.2 0.1 reshape.60
  80.3 0.1 eq.15
  80.4 0.2 slice_reduce_fusion
  80.6 0.1 iota_compare_fusion
  80.7 0.1 lt.36
  80.8 0.1 convert_reduce_fusion
  81.0 0.0 all-to-all-done
  81.0 6.5 %copy.17 = bf16[2,128,32,128]{3,0,2,1:T(2,128)(2,1)} copy(bf16[2,128,32,128]{1,0,3,2:T(2,128)(2,1)S(1)} %bitcast.36) | data formatting | bytes 4194304 | tf_op jit(solution)/shard_map/all_to_all | solution.py:42
  87.5 2.0 %convolution_divide_fusion = f32[28,128,128]{2,0,1:T(8,128)S(1)} fusion(bf16[64,128,128]{2,0,1:T(8,128)(2,1)} %bitcast.38, f32[28]{0:T(128)S(1)} %broadcast_maximum_fusion, s32[64]{0:T(128)S(1)} %eq.15, pred[64]{0:T(512)(128)(4,1)S(1)} %lt.36), kind=kOutput, calls=%fused_computation.13 | convolution fusion | flops 59182592 | bytes 3932592 | tf_op jit(solution)/shard_map/bs,sic->bic/dot_general | solution.py:43
  89.5 0.0 copy-start.2
  89.5 0.0 copy-start.3
  89.5 1.1 copy.18
  90.6 0.4 copy-done.2
  91.0 0.2 copy-done.3
  91.3 1.4 fusion.9
  92.7 3.1 %fusion.4 = bf16[64,128,128]{2,0,1:T(8,128)(2,1)S(1)} fusion(f32[28,128,128]{2,1,0:T(8,128)S(1)} %bitcast.34, s32[64]{0:T(128)S(1)} %eq.15, pred[64]{0:T(512)(128)(4,1)S(1)} %lt.36), kind=kOutput, calls=%fused_computation.7 | convolution fusion | flops 353373696 | bytes 3932480 | tf_op jit(solution)/shard_map/bs,bic->sic/dot_general | solution.py:50
  95.8 0.0 copy-done
  95.8 2.7 %copy.20 = bf16[64,128,128]{2,1,0:T(8,128)(2,1)} copy(bf16[64,128,128]{2,0,1:T(8,128)(2,1)S(1)} %fusion.4) | data formatting | bytes 4194304 | tf_op jit(solution)/shard_map/convert_element_type | solution.py:52
  98.5 5.3 %all-to-all-start.1 = ((bf16[64,128,128]{2,1,0:T(8,128)(2,1)}), bf16[64,128,128]{2,1,0:T(8,128)(2,1)S(1)}, u32[]{:S(2)}, u32[]{:S(2)}) async-start(bf16[64,128,128]{2,1,0:T(8,128)(2,1)} %copy.20), calls=%async_computation.1 | async-start | bytes 4194304 | tf_op jit(solution)/shard_map/all_to_all | solution.py:53
  103.8 45.6 %all-to-all-done.1 = bf16[64,128,128]{2,1,0:T(8,128)(2,1)S(1)} async-done(((bf16[64,128,128]{2,1,0:T(8,128)(2,1)}), bf16[64,128,128]{2,1,0:T(8,128)(2,1)S(1)}, u32[]{:S(2)}, u32[]{:S(2)}) %all-to-all-start.1) | async-done | bytes 2097184 | tf_op jit(solution)/shard_map/all_to_all | solution.py:53
  149.4 0.5 convert_bitcast_fusion
  149.9 4.4 %copy.21 = f32[2,128,32,128]{3,2,1,0:T(8,128)} copy(f32[2,128,32,128]{3,1,0,2:T(8,128)S(1)} %convert_bitcast_fusion) | data formatting | bytes 8388608 | tf_op jit(solution)/shard_map/convert_element_type | solution.py:56
  154.3 5.1 %reshape.58 = f32[1,2,128,4096]{3,2,1,0:T(8,128)} reshape(f32[2,128,32,128]{3,2,1,0:T(8,128)} %copy.21) | data formatting | bytes 8388608 | tf_op jit(solution)/shard_map/convert_element_type | solution.py:56
  159.4 0.0 copy-done.1
  159.4 4.4 %fusion.1 = bf16[1,2,128,4096]{3,2,1,0:T(8,128)(2,1)} fusion(f32[1,2,128,4096]{3,2,1,0:T(8,128)} %reshape.58, bf16[1,2,128,4096]{3,2,1,0:T(8,128)(2,1)S(1)} %copy-done.1, pred[2]{0:T(512)(128)(4,1)S(1)} %iota_compare_fusion.2), kind=kLoop, calls=%fused_computation.3 | loop fusion | flops 5242880 | bytes 8388610 | tf_op jit(solution)/shard_map/convert_element_type | solution.py:57
  (8 shorter events, 0.0 us)
Async XLA Ops:
  6.8 11.7 %copy-start.5 = (u32[256]{0:T(256)S(1)}, u32[256]{0:T(256)}, u32[]{:S(2)}) copy-start(u32[256]{0:T(256)} %constant.22) | copy-start | bytes 3076
  6.8 13.0 %copy-start.4 = (s32[1,2]{1,0:T(1,128)S(1)}, s32[1,2]{1,0:T(1,128)}, u32[]{:S(2)}) copy-start(s32[1,2]{1,0:T(1,128)} %param.10) | copy-start | bytes 28
  6.8 74.2 %all-to-all-start = ((bf16[2,128,4096]{1,0,2:T(2,128)(2,1)}), bf16[2,128,4096]{1,0,2:T(2,128)(2,1)S(1)}, u32[]{:S(2)}, u32[]{:S(2)}) async-start(bf16[2,128,4096]{1,0,2:T(2,128)(2,1)} %bitcast.37), calls=%async_computation | async-start | bytes 4194304 | tf_op jit(solution)/shard_map/all_to_all | solution.py:42
  89.5 1.5 copy-start.2
  89.5 1.7 %copy-start.3 = (bf16[3584,128]{1,0:T(8,128)(2,1)S(1)}, bf16[3584,128]{1,0:T(8,128)(2,1)}, u32[]{:S(2)}) copy-start(bf16[3584,128]{1,0:T(8,128)(2,1)} %param.7) | copy-start | bytes 2752516
  92.6 3.1 %copy-start = (f32[3584,128]{1,0:T(8,128)}, f32[3584,128]{1,0:T(8,128)S(1)}, u32[]{:S(2)}) copy-start(f32[3584,128]{1,0:T(8,128)S(1)} %get-tuple-element.4) | copy-start | bytes 5505028
  98.5 50.9 %all-to-all-start.1 = ((bf16[64,128,128]{2,1,0:T(8,128)(2,1)}), bf16[64,128,128]{2,1,0:T(8,128)(2,1)S(1)}, u32[]{:S(2)}, u32[]{:S(2)}) async-start(bf16[64,128,128]{2,1,0:T(8,128)(2,1)} %copy.20), calls=%async_computation.1 | async-start | bytes 4194304 | tf_op jit(solution)/shard_map/all_to_all | solution.py:53
  154.3 5.1 %copy-start.1 = (bf16[1,2,128,4096]{3,2,1,0:T(8,128)(2,1)S(1)}, bf16[1,2,128,4096]{3,2,1,0:T(8,128)(2,1)}, u32[]{:S(2)}) copy-start(bf16[1,2,128,4096]{3,2,1,0:T(8,128)(2,1)} %param.9) | copy-start | bytes 6291460
where the time goes:
time: 166 us; the launch traced here: 164 us
  blocking collectives  60.3 us (36%)
  waiting for transfers between devices  45.6 us (27%)
  local copies, waits for them, and re-layouts  27.7 us (17%)
  starting transfers between devices  16.3 us (10%)
  other arithmetic  6.65 us (4%)
  matrix products  5.12 us (3%)
  between operations  2.09 us (1%)
    unnamed x1, blocking collectives  60.3 us
    all_to_all x1, waiting for transfers between devices, local(): lax.all_to_all(fetched, 'replica', split_axis=0, concat_axis=2, tiled=True)  45.6 us
    all_to_all x1, starting transfers between devices, local(): lax.all_to_all(replica_deltas[0], 'replica', split_axis=2, concat_axis=0,...  11 us
    convert_element_type x2, local copies, waits for them, and re-layouts, local(): returned.astype(jnp.float32)  9.49 us
    unnamed x15, local copies, waits for them, and re-layouts  7.41 us
    all_to_all x1, local copies, waits for them, and re-layouts, local(): lax.all_to_all(replica_deltas[0], 'replica', split_axis=2, concat_axis=0,...  6.54 us
    all_to_all x1, starting transfers between devices, local(): lax.all_to_all(fetched, 'replica', split_axis=0, concat_axis=2, tiled=True)  5.29 us
    convert_element_type x1, other arithmetic, local(): blended = jnp.where(own_flags, mixed, rows_float).astype(jnp.bfloat16)  4.36 us
  transfers between devices with their start and end apart: 2, of which 1 were waited for; matrix products, arithmetic and copies ran while one was open for 1% of the time, Pallas kernels for 0%

commit v1 on v0

v1 whole, which is shorter than its diff:
```python
import functools

import jax
import jax.numpy as jnp
from jax import lax
from jax.experimental import pallas as pl
from jax.experimental.pallas import tpu as pltpu
from jax.sharding import PartitionSpec as P

outer_rate = 0.7
nesterov_decay = 0.9
blend_weight = 0.5

MESH = pl.DeviceIdType.MESH
TILE = 16
LANES = 128
RING = 8


def peer_at(k, me, n):
    kz = lax.rem(k, RING)
    far = lax.div(kz + 1, 2) * (1 - 2 * lax.rem(kz + 1, 2))
    z = lax.rem(lax.rem(me, RING) + far + RING, RING)
    y = lax.rem(lax.div(me, RING) + lax.div(k, RING), n // RING)
    return y * RING + z


def kernel(
    n, chunks, blocks,
    ids_ref, count_ref, deltas_ref, rows_ref, params_ref, momentum_ref,
    params, momentum, own,
    src, got, sel, tally, fresh, back, ret, mine, table, listed, own_ids, own_count,
    local_sem, table_sem, table_send, list_sem, send1, recv1, send2, recv2,
):
    me = lax.axis_index("replica")
    slots = src.shape[0]
    block = src.shape[1]
    rows = block // chunks
    tiles = rows // TILE
    total = n * slots
    loads = [
        pltpu.make_async_copy(a, b, local_sem.at[i])
        for i, (a, b) in enumerate(
            (
                (ids_ref, own_ids), (count_ref, own_count), (deltas_ref.at[0], src),
                (params_ref, params), (momentum_ref, momentum), (rows_ref, own),
            )
        )
    ]
    for copy in loads:
        copy.start()

    barrier = pltpu.get_barrier_semaphore()

    @pl.loop(1, n)
    def _(k):
        pl.semaphore_signal(barrier, inc=1, device_id={"replica": peer_at(k, me, n)}, device_id_type=MESH)

    loads[0].wait()
    loads[1].wait()
    first = lax.axis_index("expert") * blocks
    count = own_count[0, 0]
    lane = lax.broadcasted_iota(jnp.int32, (1, LANES), 1)
    row = jnp.full((1, LANES), -1, jnp.int32)
    for j in range(slots):
        row = jnp.where((lane == j) & (j < count), own_ids[0, j] - first, row)
    mine[...] = row
    table[me] = row
    loads[2].wait()
    pl.semaphore_wait(barrier, n - 1)

    def cols(p):
        return pl.ds(pl.multiple_of(p * LANES, LANES), LANES)

    @pl.loop(1, n)
    def _(k):
        p = peer_at(k, me, n)
        pltpu.make_async_remote_copy(
            src_ref=mine, dst_ref=table.at[me], send_sem=table_send, recv_sem=table_sem,
            device_id={"replica": p}, device_id_type=MESH,
        ).start()

    @pl.loop(0, chunks)
    def _(c):
        part = pl.ds(c * rows, rows)

        @pl.loop(1, n)
        def _(k):
            p = peer_at(k, me, n)
            pltpu.make_async_remote_copy(
                src_ref=src.at[:, part, cols(p)], dst_ref=got.at[c, me], send_sem=send1, recv_sem=recv1.at[c],
                device_id={"replica": p}, device_id_type=MESH,
            ).start()

    for c in range(chunks):
        got[c, me] = src[:, c * rows : (c + 1) * rows, cols(me)]

    rest = table.at[pl.ds(0, n - 1)]
    pltpu.make_async_copy(rest, rest, table_sem).wait()
    to_scalars = pltpu.make_async_copy(table, listed, list_sem)
    to_scalars.start()
    to_scalars.wait()
    slot_of = lax.broadcasted_iota(jnp.int32, (1, total * TILE), 1)
    inner = lax.rem(slot_of, TILE)
    slot_of = lax.div(slot_of, TILE)
    target = jnp.full((1, total * TILE), -TILE, jnp.int32)
    for s in range(total):
        target = jnp.where(slot_of == s, listed[s // slots, 0, s % slots] * TILE, target)
    target = target + inner
    at = lax.broadcasted_iota(jnp.int32, (TILE, total * TILE), 0)

    @pl.loop(0, blocks)
    def _(b):
        there = pl.ds(pl.multiple_of(b * TILE, TILE), TILE)
        sel[there, :] = jnp.where(at + b * TILE == target, 1.0, 0.0).astype(jnp.bfloat16)

    tally[...] = jnp.maximum(
        jnp.dot(sel[...], jnp.ones((total * TILE, LANES), jnp.bfloat16), preferred_element_type=jnp.float32), 1.0
    )
    loads[3].wait()
    loads[4].wait()

    @pl.loop(0, chunks)
    def _(c):
        arrived = got.at[c, pl.ds(0, n - 1)]
        pltpu.make_async_copy(arrived, arrived, recv1.at[c]).wait()

        @pl.loop(0, tiles)
        def _(t):
            inside = pl.ds(pl.multiple_of(t * TILE, TILE), TILE)
            here = pl.ds(pl.multiple_of(c * rows + t * TILE, TILE), TILE)
            tile = got[c, :, :, inside, :].reshape(total * TILE, LANES)
            totals = jnp.dot(sel[...], tile, preferred_element_type=jnp.float32)
            mean = totals / tally[...]
            moment = nesterov_decay * momentum[:, here, :].reshape(blocks * TILE, LANES).astype(jnp.float32) + mean
            fresh_tile = params[:, here, :].reshape(blocks * TILE, LANES) - outer_rate * (
                mean + nesterov_decay * moment
            )
            params[:, here, :] = fresh_tile.reshape(blocks, TILE, LANES)
            momentum[:, here, :] = moment.astype(jnp.bfloat16).reshape(blocks, TILE, LANES)
            fresh[:, inside, :] = fresh_tile.astype(jnp.bfloat16).reshape(blocks, TILE, LANES)

        part = pl.ds(pl.multiple_of(c * rows, TILE), rows)
        for s in range(total):
            back[c, s // slots, s % slots] = fresh[jnp.maximum(listed[s // slots, 0, s % slots], 0)]

        for j in range(slots):
            ret[j, part, cols(me)] = fresh[jnp.maximum(listed[me, 0, j], 0)]

        @pl.loop(1, n)
        def _(k):
            p = peer_at(k, me, n)
            pltpu.make_async_remote_copy(
                src_ref=back.at[c, p], dst_ref=ret.at[:, part, cols(me)], send_sem=send2, recv_sem=recv2.at[c],
                device_id={"replica": p}, device_id_type=MESH,
            ).start()

    loads[5].wait()

    @pl.loop(0, chunks)
    def _(c):
        arrived = got.at[c, pl.ds(0, n - 1)]
        pltpu.make_async_copy(arrived, arrived, recv2.at[c]).wait()
        part = pl.ds(pl.multiple_of(c * rows, TILE), rows)
        for j in range(slots):

            @pl.loop(0, n)
            def _(q):
                old = own[0, j, part, cols(q)].astype(jnp.float32)
                new = ret[j, part, cols(q)].astype(jnp.float32)
                mixed = blend_weight * old + (1.0 - blend_weight) * new
                own[0, j, part, cols(q)] = jnp.where(j < count, mixed, old).astype(jnp.bfloat16)


    pltpu.make_async_copy(rest, rest, table_send).wait()
    sent = got.at[:, pl.ds(0, n - 1)]
    pltpu.make_async_copy(sent, sent, send1).wait()
    pltpu.make_async_copy(sent, sent, send2).wait()


def write_out(params, momentum, own, params_out, momentum_out, blended_out, sem):
    copies = [
        pltpu.make_async_copy(a, b, sem.at[i])
        for i, (a, b) in enumerate(((params, params_out), (own, blended_out), (momentum, momentum_out)))
    ]
    for copy in copies:
        copy.start()
    for copy in copies:
        copy.wait()


def local(outer_params, momentum, replica_deltas, replica_rows, block_ids, slot_counts):
    n = lax.axis_size("replica")
    _, slots, block, width = replica_deltas.shape
    blocks = outer_params.shape[0] // block
    slab = outer_params.shape[1]
    total = n * slots
    chunks = 4
    rows = block // chunks
    f32, bf16 = jnp.float32, jnp.bfloat16
    hbm = pl.BlockSpec(memory_space=pltpu.HBM)
    vmem = pl.BlockSpec(memory_space=pltpu.VMEM)
    dma = pltpu.SemaphoreType.DMA
    results = (
        jax.ShapeDtypeStruct((blocks, block, slab), f32),
        jax.ShapeDtypeStruct((blocks, block, slab), bf16),
        jax.ShapeDtypeStruct(replica_rows.shape, bf16),
    )
    held = pl.pallas_call(
        functools.partial(kernel, n, chunks, blocks),
        out_shape=results,
        in_specs=[hbm] * 6,
        out_specs=(vmem,) * 3,
        scratch_shapes=[
            pltpu.VMEM((slots, block, width), bf16),
            pltpu.VMEM((chunks, n, slots, rows, slab), bf16),
            pltpu.VMEM((blocks * TILE, total * TILE), bf16),
            pltpu.VMEM((blocks * TILE, slab), f32),
            pltpu.VMEM((blocks, rows, slab), bf16),
            pltpu.VMEM((chunks, n, slots, rows, slab), bf16),
            pltpu.VMEM((slots, block, width), bf16),
            pltpu.VMEM((1, LANES), jnp.int32),
            pltpu.VMEM((n, 1, LANES), jnp.int32),
            pltpu.SMEM((n, 1, LANES), jnp.int32),
            pltpu.SMEM((1, slots), jnp.int32),
            pltpu.SMEM((1, 1), jnp.int32),
            dma((6,)), dma, dma, dma, dma, dma((chunks,)), dma, dma((chunks,)),
        ],
        compiler_params=pltpu.CompilerParams(
            collective_id=0, has_side_effects=True, vmem_limit_bytes=32 * 1024 * 1024
        ),
        cost_estimate=pl.CostEstimate(flops=10**9, bytes_accessed=13 * 10**6, transcendentals=0),
    )(
        *(
            pltpu.with_memory_space_constraint(a, pltpu.HBM) if a.size > 1 else a
            for a in (
                block_ids, slot_counts, replica_deltas, replica_rows,
                outer_params.reshape(blocks, block, slab), momentum.reshape(blocks, block, slab),
            )
        ),
    )
    new_params, new_momentum, blended = pl.pallas_call(
        write_out,
        out_shape=results,
        in_specs=[vmem] * 3,
        out_specs=(hbm,) * 3,
        scratch_shapes=[dma((3,))],
        compiler_params=pltpu.CompilerParams(vmem_limit_bytes=16 * 1024 * 1024),
    )(*held)
    return new_params.reshape(outer_params.shape), new_momentum.reshape(momentum.shape), blended


def solution(mesh):
    in_specs = (
        P("expert", "replica"),
        P("expert", "replica"),
        P("replica", "expert", None, None),
        P("replica", "expert", None, None),
        P("replica", "expert"),
        P("replica", "expert"),
    )
    out_specs = (P("expert", "replica"), P("expert", "replica"), P("replica", "expert", None, None))
    return jax.shard_map(local, mesh=mesh, in_specs=in_specs, out_specs=out_specs, check_vma=False)
```

time: 166 us -> 107 us (0.64)
  Pallas kernels: 0 us -> 104 us
  blocking collectives: 60.3 us -> 0 us
  waiting for transfers between devices: 45.6 us -> 0 us
  local copies, waits for them, and re-layouts: 27.7 us -> 0 us
  starting transfers between devices: 16.3 us -> 0 us
  other arithmetic: 6.65 us -> 0 us
  matrix products: 5.12 us -> 0 us
    pallas_call x0 -> x2, Pallas kernels: none -> 104 us  [the longest x1 102 us: local(): pl.pallas_call(functools.partial(kernel, n, chunks, blocks), out_shape=re...]
    unnamed x1 -> x0, blocking collectives: 60.3 us -> none
    all_to_all x2 -> x0, waiting for transfers between devices: 45.6 us -> none  [the longest x1 45.6 us: local(): lax.all_to_all(fetched, 'replica', split_axis=0, concat_axis=2, tiled=True)]
    all_to_all x2 -> x0, starting transfers between devices: 16.3 us -> none  [the longest x1 11 us: local(): lax.all_to_all(replica_deltas[0], 'replica', split_axis=2, concat_axis=0,...]
    convert_element_type x3 -> x0, local copies, waits for them, and re-layouts: 12.2 us -> none  [the longest x2 9.49 us: local(): returned.astype(jnp.float32)]
    unnamed x15 -> x0, local copies, waits for them, and re-layouts: 7.41 us -> none
    all_to_all x1 -> x0, local copies, waits for them, and re-layouts: 6.54 us -> none  [local(): lax.all_to_all(replica_deltas[0], 'replica', split_axis=2, concat_axis=0,...]
    convert_element_type x3 -> x0, other arithmetic: 6.27 us -> none  [the longest x1 4.36 us: local(): blended = jnp.where(own_flags, mixed, rows_float).astype(jnp.bfloat16)]
  transfers between devices with their start and end apart: 2 -> 0, of which waited for: 1 -> 0; matrix products, arithmetic and copies ran while one was open for 1% -> 0% of each run, Pallas kernels for 0% -> 0%
where the time goes in v1:
time: 107 us; the launch traced here: 106 us
  Pallas kernels  104 us (97%)
  between operations  1.29 us (1%)
    pallas_call x1, Pallas kernels, local(): pl.pallas_call(functools.partial(kernel, n, chunks, blocks), out_shape=re...  102 us
    pallas_call x1, Pallas kernels, local(): pl.pallas_call(write_out, out_shape=results, in_specs=[vmem] * 3, out_spe...  2.24 us

profile of v1, /device:TPU:64, one launch (start us, length us, event | category | flops | bytes accessed | tf_op | source)
XLA Modules:
  0.0 105.6 jit_solution(2881154088653414749)
XLA Ops:
  1.3 102.0 %shard_map.85 = (f32[28,128,128]{2,1,0:T(8,128)S(1)}, bf16[28,128,128]{2,1,0:T(8,128)(2,1)S(1)}, bf16[1,2,128,4096]{3,2,1,0:T(8,128)(2,1)S(1)}) custom-call(s32[1,2]{1,0:T(1,128)} %ids_ref.1, s32[1,1]{1,0:T(1,128)S(6)} %copy.9.count_ref, bf16[1,2,128,4096]{3,2,1,0:T(8,128)(2,1)} %deltas_ref.1, bf16[1,2,128,4096]{3,2,1,0:T(8,128)(2,1)} %rows_ref.1, ...), custom_call_target="tpu_custom_call" | custom-call | flops 1000000000 | bytes 13000000 | tf_op jit(solution)/shard_map/pallas_call | solution.py:209
  103.3 2.2 %shard_map.86 = (f32[28,128,128]{2,1,0:T(8,128)}, bf16[28,128,128]{2,1,0:T(8,128)(2,1)}, bf16[1,2,128,4096]{3,2,1,0:T(8,128)(2,1)}) custom-call(f32[28,128,128]{2,1,0:T(8,128)S(1)} %get-tuple-element.9.params, bf16[28,128,128]{2,1,0:T(8,128)(2,1)S(1)} %get-tuple-element.10.momentum, bf16[1,2,128,4096]{3,2,1,0:T(8,128)(2,1)S(1)} %get-tuple-element.11.own), custom_call_target="tpu_custom_call" | custom-call | tf_op jit(solution)/shard_map/pallas_call | solution.py:242

commit v2 on v1

--- a/solution.py
+++ b/solution.py
@@ -17,12 +17,23 @@
 RING = 8
 
 
-def peer_at(k, me, n):
-    kz = lax.rem(k, RING)
-    far = lax.div(kz + 1, 2) * (1 - 2 * lax.rem(kz + 1, 2))
-    z = lax.rem(lax.rem(me, RING) + far + RING, RING)
-    y = lax.rem(lax.div(me, RING) + lax.div(k, RING), n // RING)
+GROUPS = 5
+
+
+def peer_in(g, i, me, n):
+    if g == 0:
+        dy, dz = i + 1, 0
+    elif g == GROUPS - 1:
+        dy, dz = i, g
+    else:
+        dy, dz = lax.div(i, 2), g * (1 - 2 * lax.rem(i, 2))
+    z = lax.rem(lax.rem(me, RING) + dz + RING, RING)
+    y = lax.rem(lax.div(me, RING) + dy, n // RING)
     return y * RING + z
+
+
+def group_size(g, n):
+    return (n // RING - 1, 2 * (n // RING), 2 * (n // RING), 2 * (n // RING), n // RING)[g]
 
 
 def kernel(
@@ -30,7 +41,7 @@
     ids_ref, count_ref, deltas_ref, rows_ref, params_ref, momentum_ref,
     params, momentum, own,
     src, got, sel, tally, fresh, back, ret, mine, table, listed, own_ids, own_count,
-    local_sem, table_sem, table_send, list_sem, send1, recv1, send2, recv2,
+    local_sem, known, table_sem, table_send, list_sem, send1, recv1, send2, recv2,
 ):
     me = lax.axis_index("replica")
     slots = src.shape[0]
@@ -52,9 +63,13 @@
 
     barrier = pltpu.get_barrier_semaphore()
 
-    @pl.loop(1, n)
-    def _(k):
-        pl.semaphore_signal(barrier, inc=1, device_id={"replica": peer_at(k, me, n)}, device_id_type=MESH)
+    for g in (0, 1):
+
+        @pl.loop(0, group_size(g, n))
+        def _(i):
+            pl.semaphore_signal(
+                barrier, inc=1, device_id={"replica": peer_in(g, i, me, n)}, device_id_type=MESH
+            )
 
     loads[0].wait()
     loads[1].wait()
@@ -67,30 +82,49 @@
     mine[...] = row
     table[me] = row
     loads[2].wait()
-    pl.semaphore_wait(barrier, n - 1)
+    pl.semaphore_wait(barrier, group_size(0, n) + group_size(1, n))
 
     def cols(p):
         return pl.ds(pl.multiple_of(p * LANES, LANES), LANES)
 
-    @pl.loop(1, n)
-    def _(k):
-        p = peer_at(k, me, n)
-        pltpu.make_async_remote_copy(
-            src_ref=mine, dst_ref=table.at[me], send_sem=table_send, recv_sem=table_sem,
-            device_id={"replica": p}, device_id_type=MESH,
-        ).start()
-
-    @pl.loop(0, chunks)
-    def _(c):
+    def tell(level):
+        for away in (1, RING - 1):
+            z = lax.rem(lax.rem(me, RING) + away, RING)
+            pl.semaphore_signal(
+                known.at[level], inc=1, device_id={"replica": lax.div(me, RING) * RING + z}, device_id_type=MESH
+            )
+
+    def send_table(g):
+        @pl.loop(0, group_size(g, n))
+        def _(i):
+            pltpu.make_async_remote_copy(
+                src_ref=mine, dst_ref=table.at[me], send_sem=table_send, recv_sem=table_sem,
+                device_id={"replica": peer_in(g, i, me, n)}, device_id_type=MESH,
+            ).start()
+
+    def send_slab(c, g):
         part = pl.ds(c * rows, rows)
 
-        @pl.loop(1, n)
-        def _(k):
-            p = peer_at(k, me, n)
+        @pl.loop(0, group_size(g, n))
+        def _(i):
+            p = peer_in(g, i, me, n)
             pltpu.make_async_remote_copy(
                 src_ref=src.at[:, part, cols(p)], dst_ref=got.at[c, me], send_sem=send1, recv_sem=recv1.at[c],
                 device_id={"replica": p}, device_id_type=MESH,
             ).start()
+
+    for g in range(GROUPS):
+        if g > 1:
+            pl.semaphore_wait(known.at[g - 2], 2)
+        if 0 < g < GROUPS - 1:
+            tell(g - 1)
+        send_table(g)
+        send_slab(0, g)
+
+    @pl.loop(1, chunks)
+    def _(c):
+        for g in range(GROUPS):
+            send_slab(c, g)
 
     for c in range(chunks):
         got[c, me] = src[:, c * rows : (c + 1) * rows, cols(me)]
@@ -147,13 +181,15 @@
         for j in range(slots):
             ret[j, part, cols(me)] = fresh[jnp.maximum(listed[me, 0, j], 0)]
 
-        @pl.loop(1, n)
-        def _(k):
-            p = peer_at(k, me, n)
-            pltpu.make_async_remote_copy(
-                src_ref=back.at[c, p], dst_ref=ret.at[:, part, cols(me)], send_sem=send2, recv_sem=recv2.at[c],
-                device_id={"replica": p}, device_id_type=MESH,
-            ).start()
+        for g in reversed(range(GROUPS)):
+
+            @pl.loop(0, group_size(g, n))
+            def _(i):
+                p = peer_in(g, i, me, n)
+                pltpu.make_async_remote_copy(
+                    src_ref=back.at[c, p], dst_ref=ret.at[:, part, cols(me)], send_sem=send2, recv_sem=recv2.at[c],
+                    device_id={"replica": p}, device_id_type=MESH,
+                ).start()
 
     loads[5].wait()
 
@@ -195,7 +231,7 @@
     blocks = outer_params.shape[0] // block
     slab = outer_params.shape[1]
     total = n * slots
-    chunks = 4
+    chunks = 2
     rows = block // chunks
     f32, bf16 = jnp.float32, jnp.bfloat16
     hbm = pl.BlockSpec(memory_space=pltpu.HBM)
@@ -224,7 +260,7 @@
             pltpu.SMEM((n, 1, LANES), jnp.int32),
             pltpu.SMEM((1, slots), jnp.int32),
             pltpu.SMEM((1, 1), jnp.int32),
-            dma((6,)), dma, dma, dma, dma, dma((chunks,)), dma, dma((chunks,)),
+            dma((6,)), pltpu.SemaphoreType.REGULAR((GROUPS - 2,)), dma, dma, dma, dma, dma((chunks,)), dma, dma((chunks,)),
         ],
         compiler_params=pltpu.CompilerParams(
             collective_id=0, has_side_effects=True, vmem_limit_bytes=32 * 1024 * 1024

time: 107 us -> 106 us (level)
    pallas_call x1, Pallas kernels: 102 us -> 100 us  [local(): pl.pallas_call(functools.partial(kernel, n, chunks, blocks), out_shape=re...]
where the time goes in v2:
time: 106 us; the launch traced here: 104 us
  Pallas kernels  103 us (97%)
  between operations  1.29 us (1%)
    pallas_call x1, Pallas kernels, local(): pl.pallas_call(functools.partial(kernel, n, chunks, blocks), out_shape=re...  100 us
    pallas_call x1, Pallas kernels, local(): pl.pallas_call(write_out, out_shape=results, in_specs=[vmem] * 3, out_spe...  2.24 us

profile of v2, /device:TPU:64, one launch (start us, length us, event | category | flops | bytes accessed | tf_op | source)
XLA Modules:
  0.0 103.8 jit_solution(12949586081443039363)
XLA Ops:
  1.3 100.3 %shard_map.85 = (f32[28,128,128]{2,1,0:T(8,128)S(1)}, bf16[28,128,128]{2,1,0:T(8,128)(2,1)S(1)}, bf16[1,2,128,4096]{3,2,1,0:T(8,128)(2,1)S(1)}) custom-call(s32[1,2]{1,0:T(1,128)} %ids_ref.1, s32[1,1]{1,0:T(1,128)S(6)} %copy.9.count_ref, bf16[1,2,128,4096]{3,2,1,0:T(8,128)(2,1)} %deltas_ref.1, bf16[1,2,128,4096]{3,2,1,0:T(8,128)(2,1)} %rows_ref.1, ...), custom_call_target="tpu_custom_call" | custom-call | flops 1000000000 | bytes 13000000 | tf_op jit(solution)/shard_map/pallas_call | solution.py:245
  101.6 2.2 %shard_map.86 = (f32[28,128,128]{2,1,0:T(8,128)}, bf16[28,128,128]{2,1,0:T(8,128)(2,1)}, bf16[1,2,128,4096]{3,2,1,0:T(8,128)(2,1)}) custom-call(f32[28,128,128]{2,1,0:T(8,128)S(1)} %get-tuple-element.9.params, bf16[28,128,128]{2,1,0:T(8,128)(2,1)S(1)} %get-tuple-element.10.momentum, bf16[1,2,128,4096]{3,2,1,0:T(8,128)(2,1)S(1)} %get-tuple-element.11.own), custom_call_target="tpu_custom_call" | custom-call | tf_op jit(solution)/shard_map/pallas_call | solution.py:278

commit v3 on v2

--- a/solution.py
+++ b/solution.py
@@ -36,11 +36,17 @@
     return (n // RING - 1, 2 * (n // RING), 2 * (n // RING), 2 * (n // RING), n // RING)[g]
 
 
+def blend(rows, fetched, live):
+    old = rows.astype(jnp.float32)
+    mixed = blend_weight * old + (1.0 - blend_weight) * fetched.astype(jnp.float32)
+    return jnp.where(live, mixed, old).astype(jnp.bfloat16)
+
+
 def kernel(
     n, chunks, blocks,
     ids_ref, count_ref, deltas_ref, rows_ref, params_ref, momentum_ref,
-    params, momentum, own,
-    src, got, sel, tally, fresh, back, ret, mine, table, listed, own_ids, own_count,
+    params, momentum, own, ret,
+    src, got, sel, tally, fresh, back, mine, table, listed, own_ids, own_count,
     local_sem, known, table_sem, table_send, list_sem, send1, recv1, send2, recv2,
 ):
     me = lax.axis_index("replica")
@@ -49,17 +55,14 @@
     rows = block // chunks
     tiles = rows // TILE
     total = n * slots
-    loads = [
-        pltpu.make_async_copy(a, b, local_sem.at[i])
-        for i, (a, b) in enumerate(
-            (
-                (ids_ref, own_ids), (count_ref, own_count), (deltas_ref.at[0], src),
-                (params_ref, params), (momentum_ref, momentum), (rows_ref, own),
-            )
-        )
-    ]
-    for copy in loads:
-        copy.start()
+    parts = [pl.ds(c * rows, rows) for c in range(chunks)]
+    pairs = (
+        [(ids_ref, own_ids), (count_ref, own_count)]
+        + [(deltas_ref.at[0, :, part], src.at[:, part]) for part in parts]
+        + [(params_ref, params), (momentum_ref, momentum), (rows_ref, own)]
+    )
+    loads = [pltpu.make_async_copy(a, b, local_sem.at[i]) for i, (a, b) in enumerate(pairs)]
+    urgent, deltas_loads, later = loads[:2], loads[2:-3], loads[-3:]
 
     barrier = pltpu.get_barrier_semaphore()
 
@@ -71,8 +74,10 @@
                 barrier, inc=1, device_id={"replica": peer_in(g, i, me, n)}, device_id_type=MESH
             )
 
-    loads[0].wait()
-    loads[1].wait()
+    for copy in urgent + deltas_loads:
+        copy.start()
+    for copy in urgent:
+        copy.wait()
     first = lax.axis_index("expert") * blocks
     count = own_count[0, 0]
     lane = lax.broadcasted_iota(jnp.int32, (1, LANES), 1)
@@ -81,7 +86,7 @@
         row = jnp.where((lane == j) & (j < count), own_ids[0, j] - first, row)
     mine[...] = row
     table[me] = row
-    loads[2].wait()
+    deltas_loads[0].wait()
     pl.semaphore_wait(barrier, group_size(0, n) + group_size(1, n))
 
     def cols(p):
@@ -121,11 +126,13 @@
         send_table(g)
         send_slab(0, g)
 
-    @pl.loop(1, chunks)
-    def _(c):
+    for c in range(1, chunks):
+        deltas_loads[c].wait()
         for g in range(GROUPS):
             send_slab(c, g)
 
+    for copy in later:
+        copy.start()
     for c in range(chunks):
         got[c, me] = src[:, c * rows : (c + 1) * rows, cols(me)]
 
@@ -151,8 +158,8 @@
     tally[...] = jnp.maximum(
         jnp.dot(sel[...], jnp.ones((total * TILE, LANES), jnp.bfloat16), preferred_element_type=jnp.float32), 1.0
     )
-    loads[3].wait()
-    loads[4].wait()
+    later[0].wait()
+    later[1].wait()
 
     @pl.loop(0, chunks)
     def _(c):
@@ -181,47 +188,71 @@
         for j in range(slots):
             ret[j, part, cols(me)] = fresh[jnp.maximum(listed[me, 0, j], 0)]
 
-        for g in reversed(range(GROUPS)):
-
+        def send_back(g, wanted):
             @pl.loop(0, group_size(g, n))
             def _(i):
                 p = peer_in(g, i, me, n)
-                pltpu.make_async_remote_copy(
-                    src_ref=back.at[c, p], dst_ref=ret.at[:, part, cols(me)], send_sem=send2, recv_sem=recv2.at[c],
-                    device_id={"replica": p}, device_id_type=MESH,
-                ).start()
-
-    loads[5].wait()
-
-    @pl.loop(0, chunks)
-    def _(c):
+
+                @pl.when(wanted(lax.rem(p, RING)))
+                def _():
+                    pltpu.make_async_remote_copy(
+                        src_ref=back.at[c, p], dst_ref=ret.at[:, part, cols(me)], send_sem=send2,
+                        recv_sem=recv2.at[c], device_id={"replica": p}, device_id_type=MESH,
+                    ).start()
+
+        for low, high in ((0, 1), (1, 2), (2, 3), (3, 4), (4, 8)):
+            for g in reversed(range(GROUPS)):
+                send_back(g, lambda z: (low <= z) & (z < high))
+
+    later[2].wait()
+
+    def wait_back(c):
         arrived = got.at[c, pl.ds(0, n - 1)]
         pltpu.make_async_copy(arrived, arrived, recv2.at[c]).wait()
+
+    @pl.loop(0, chunks - 1)
+    def _(c):
+        wait_back(c)
         part = pl.ds(pl.multiple_of(c * rows, TILE), rows)
         for j in range(slots):
 
             @pl.loop(0, n)
             def _(q):
-                old = own[0, j, part, cols(q)].astype(jnp.float32)
-                new = ret[j, part, cols(q)].astype(jnp.float32)
-                mixed = blend_weight * old + (1.0 - blend_weight) * new
-                own[0, j, part, cols(q)] = jnp.where(j < count, mixed, old).astype(jnp.bfloat16)
-
-
+                own[0, j, part, cols(q)] = blend(own[0, j, part, cols(q)], ret[j, part, cols(q)], j < count)
+
+    wait_back(chunks - 1)
     pltpu.make_async_copy(rest, rest, table_send).wait()
     sent = got.at[:, pl.ds(0, n - 1)]
     pltpu.make_async_copy(sent, sent, send1).wait()
     pltpu.make_async_copy(sent, sent, send2).wait()
 
 
-def write_out(params, momentum, own, params_out, momentum_out, blended_out, sem):
-    copies = [
-        pltpu.make_async_copy(a, b, sem.at[i])
-        for i, (a, b) in enumerate(((params, params_out), (own, blended_out), (momentum, momentum_out)))
-    ]
-    for copy in copies:
+def write_out(
+    start, pieces, count_ref, params, momentum, own, ret, params_out, momentum_out, blended_out, mixed, sem
+):
+    count = count_ref[0, 0]
+    done = [pltpu.make_async_copy(params, params_out, sem.at[0]), pltpu.make_async_copy(momentum, momentum_out, sem.at[1])]
+    if start:
+        ready = pl.ds(0, start)
+        done.append(pltpu.make_async_copy(own.at[:, :, ready], blended_out.at[:, :, ready], sem.at[2]))
+    for copy in done:
         copy.start()
-    for copy in copies:
+    slots, block, width = own.shape[1:]
+    rows = (block - start) // pieces
+    for p in range(pieces):
+        for j in range(slots):
+            here = pl.ds(start + p * rows, rows)
+            there = pl.ds(p * rows, rows)
+
+            @pl.loop(0, width // LANES)
+            def _(q):
+                at = pl.ds(pl.multiple_of(q * LANES, LANES), LANES)
+                mixed[j, there, at] = blend(own[0, j, here, at], ret[j, here, at], j < count)
+
+            copy = pltpu.make_async_copy(mixed.at[j, there], blended_out.at[0, j, here], sem.at[3 + p * slots + j])
+            copy.start()
+            done.append(copy)
+    for copy in done:
         copy.wait()
 
 
@@ -232,6 +263,7 @@
     slab = outer_params.shape[1]
     total = n * slots
     chunks = 2
+    pieces = 2
     rows = block // chunks
     f32, bf16 = jnp.float32, jnp.bfloat16
     hbm = pl.BlockSpec(memory_space=pltpu.HBM)
@@ -244,9 +276,9 @@
     )
     held = pl.pallas_call(
         functools.partial(kernel, n, chunks, blocks),
-        out_shape=results,
+        out_shape=results + (jax.ShapeDtypeStruct((slots, block, width), bf16),),
         in_specs=[hbm] * 6,
-        out_specs=(vmem,) * 3,
+        out_specs=(vmem,) * 4,
         scratch_shapes=[
             pltpu.VMEM((slots, block, width), bf16),
             pltpu.VMEM((chunks, n, slots, rows, slab), bf16),
@@ -254,13 +286,12 @@
             pltpu.VMEM((blocks * TILE, slab), f32),
             pltpu.VMEM((blocks, rows, slab), bf16),
             pltpu.VMEM((chunks, n, slots, rows, slab), bf16),
-            pltpu.VMEM((slots, block, width), bf16),
             pltpu.VMEM((1, LANES), jnp.int32),
             pltpu.VMEM((n, 1, LANES), jnp.int32),
             pltpu.SMEM((n, 1, LANES), jnp.int32),
             pltpu.SMEM((1, slots), jnp.int32),
             pltpu.SMEM((1, 1), jnp.int32),
-            dma((6,)), pltpu.SemaphoreType.REGULAR((GROUPS - 2,)), dma, dma, dma, dma, dma((chunks,)), dma, dma((chunks,)),
+            dma((5 + chunks,)), pltpu.SemaphoreType.REGULAR((GROUPS - 2,)), dma, dma, dma, dma, dma((chunks,)), dma, dma((chunks,)),
         ],
         compiler_params=pltpu.CompilerParams(
             collective_id=0, has_side_effects=True, vmem_limit_bytes=32 * 1024 * 1024
@@ -276,13 +307,13 @@
         ),
     )
     new_params, new_momentum, blended = pl.pallas_call(
-        write_out,
+        functools.partial(write_out, block - rows, pieces),
         out_shape=results,
-        in_specs=[vmem] * 3,
+        in_specs=[pl.BlockSpec(memory_space=pltpu.SMEM)] + [vmem] * 4,
         out_specs=(hbm,) * 3,
-        scratch_shapes=[dma((3,))],
+        scratch_shapes=[pltpu.VMEM((slots, rows, width), bf16), dma((3 + slots * pieces,))],
         compiler_params=pltpu.CompilerParams(vmem_limit_bytes=16 * 1024 * 1024),
-    )(*held)
+    )(slot_counts, *held)
     return new_params.reshape(outer_params.shape), new_momentum.reshape(momentum.shape), blended
 
 

time: 106 us -> 104 us (0.981); the launches traced: 104 us -> 104 us
  no operation moved by 1% of the time
where the time goes in v3:
time: 104 us
  Pallas kernels  102 us (98%)
  between operations  1.29 us (1%)
    pallas_call x1, Pallas kernels, local(): pl.pallas_call(functools.partial(kernel, n, chunks, blocks), out_shape=re...  100 us
    pallas_call x1, Pallas kernels, local(): pl.pallas_call(functools.partial(write_out, block - rows, pieces), out_sh...  2.29 us

profile of v3, /device:TPU:64, one launch (start us, length us, event | category | flops | bytes accessed | tf_op | source)
XLA Modules:
  0.0 103.7 jit_solution(726542000696230452)
XLA Ops:
  1.3 100.1 %shard_map.85 = (f32[28,128,128]{2,1,0:T(8,128)S(1)}, bf16[28,128,128]{2,1,0:T(8,128)(2,1)S(1)}, bf16[1,2,128,4096]{3,2,1,0:T(8,128)(2,1)S(1)}, bf16[2,128,4096]{2,1,0:T(8,128)(2,1)S(1)}) custom-call(s32[1,2]{1,0:T(1,128)} %ids_ref.1, s32[1,1]{1,0:T(1,128)S(6)} %copy.9.count_ref, bf16[1,2,128,4096]{3,2,1,0:T(8,128)(2,1)} %deltas_ref.1, ...), custom_call_target="tpu_custom_call" | custom-call | flops 1000000000 | bytes 13000000 | tf_op jit(solution)/shard_map/pallas_call | solution.py:277
  101.4 2.3 %shard_map.86 = (f32[28,128,128]{2,1,0:T(8,128)}, bf16[28,128,128]{2,1,0:T(8,128)(2,1)}, bf16[1,2,128,4096]{3,2,1,0:T(8,128)(2,1)}) custom-call(s32[1,1]{1,0:T(1,128)S(6)} %copy.9.count_ref, f32[28,128,128]{2,1,0:T(8,128)S(1)} %get-tuple-element.10.params, bf16[28,128,128]{2,1,0:T(8,128)(2,1)S(1)} %get-tuple-element.11.momentum, ...), custom_call_target="tpu_custom_call" | custom-call | tf_op jit(solution)/shard_map/pallas_call | solution.py:309

commit v4 on v3

--- a/solution.py
+++ b/solution.py
@@ -193,16 +193,17 @@
             def _(i):
                 p = peer_in(g, i, me, n)
 
-                @pl.when(wanted(lax.rem(p, RING)))
+                @pl.when(wanted(lax.rem(p, RING), lax.div(p, RING)))
                 def _():
                     pltpu.make_async_remote_copy(
                         src_ref=back.at[c, p], dst_ref=ret.at[:, part, cols(me)], send_sem=send2,
                         recv_sem=recv2.at[c], device_id={"replica": p}, device_id_type=MESH,
                     ).start()
 
-        for low, high in ((0, 1), (1, 2), (2, 3), (3, 4), (4, 8)):
-            for g in reversed(range(GROUPS)):
-                send_back(g, lambda z: (low <= z) & (z < high))
+        for low, high in ((0, 1), (1, 2), (2, 3), (3, 4), (4, RING)):
+            for start, stop in ((0, 1), (1, n // RING)) if high <= RING // 2 else ((0, n // RING),):
+                for g in reversed(range(GROUPS)):
+                    send_back(g, lambda z, y: (low <= z) & (z < high) & (start <= y) & (y < stop))
 
     later[2].wait()
 

time: 104 us -> 103 us (level)
  no operation moved by 1% of the time
where the time goes in v4:
time: 103 us
  Pallas kernels  102 us (99%)
  between operations  1.29 us (1%)
    pallas_call x1, Pallas kernels, local(): pl.pallas_call(functools.partial(kernel, n, chunks, blocks), out_shape=re...  99.3 us
    pallas_call x1, Pallas kernels, local(): pl.pallas_call(functools.partial(write_out, block - rows, pieces), out_sh...  2.29 us

profile of v4, /device:TPU:64, one launch (start us, length us, event | category | flops | bytes accessed | tf_op | source)
XLA Modules:
  0.0 102.8 jit_solution(9414612755482132357)
XLA Ops:
  1.3 99.3 %shard_map.85 = (f32[28,128,128]{2,1,0:T(8,128)S(1)}, bf16[28,128,128]{2,1,0:T(8,128)(2,1)S(1)}, bf16[1,2,128,4096]{3,2,1,0:T(8,128)(2,1)S(1)}, bf16[2,128,4096]{2,1,0:T(8,128)(2,1)S(1)}) custom-call(s32[1,2]{1,0:T(1,128)} %ids_ref.1, s32[1,1]{1,0:T(1,128)S(6)} %copy.9.count_ref, bf16[1,2,128,4096]{3,2,1,0:T(8,128)(2,1)} %deltas_ref.1, ...), custom_call_target="tpu_custom_call" | custom-call | flops 1000000000 | bytes 13000000 | tf_op jit(solution)/shard_map/pallas_call | solution.py:278
  100.5 2.3 %shard_map.86 = (f32[28,128,128]{2,1,0:T(8,128)}, bf16[28,128,128]{2,1,0:T(8,128)(2,1)}, bf16[1,2,128,4096]{3,2,1,0:T(8,128)(2,1)}) custom-call(s32[1,1]{1,0:T(1,128)S(6)} %copy.9.count_ref, f32[28,128,128]{2,1,0:T(8,128)S(1)} %get-tuple-element.10.params, bf16[28,128,128]{2,1,0:T(8,128)(2,1)S(1)} %get-tuple-element.11.momentum, ...), custom_call_target="tpu_custom_call" | custom-call | tf_op jit(solution)/shard_map/pallas_call | solution.py:310

commit v5 on v3

--- a/solution.py
+++ b/solution.py
@@ -193,16 +193,21 @@
             def _(i):
                 p = peer_in(g, i, me, n)
 
-                @pl.when(wanted(lax.rem(p, RING)))
+                @pl.when(wanted(lax.rem(p, RING), lax.div(p, RING)))
                 def _():
                     pltpu.make_async_remote_copy(
                         src_ref=back.at[c, p], dst_ref=ret.at[:, part, cols(me)], send_sem=send2,
                         recv_sem=recv2.at[c], device_id={"replica": p}, device_id_type=MESH,
                     ).start()
 
-        for low, high in ((0, 1), (1, 2), (2, 3), (3, 4), (4, 8)):
+        y_all = n // RING
+        classes = (
+            (0, 1, 0, 1), (0, 1, 1, y_all), (2, 3, 0, 2), (1, 2, 0, 1), (1, 2, 1, y_all), (2, 3, 2, y_all),
+            (3, 4, 0, 1), (3, 4, 1, y_all), (4, RING, 0, y_all),
+        )
+        for low, high, start, stop in classes:
             for g in reversed(range(GROUPS)):
-                send_back(g, lambda z: (low <= z) & (z < high))
+                send_back(g, lambda z, y: (low <= z) & (z < high) & (start <= y) & (y < stop))
 
     later[2].wait()
 

time: 104 us -> 103 us (level)
  the two profiles are of different devices: /device:TPU:64 before, /device:TPU:92 now
where the time goes in v5:
time: 103 us
  Pallas kernels  102 us (99%)
  between operations  1.29 us (1%)
    pallas_call x1, Pallas kernels, local(): pl.pallas_call(functools.partial(kernel, n, chunks, blocks), out_shape=re...  99.7 us
    pallas_call x1, Pallas kernels, local(): pl.pallas_call(functools.partial(write_out, block - rows, pieces), out_sh...  2.29 us

profile of v5, /device:TPU:92, one launch (start us, length us, event | category | flops | bytes accessed | tf_op | source)
XLA Modules:
  0.0 103.3 jit_solution(5774662170067189075)
XLA Ops:
  1.3 99.7 %shard_map.85 = (f32[28,128,128]{2,1,0:T(8,128)S(1)}, bf16[28,128,128]{2,1,0:T(8,128)(2,1)S(1)}, bf16[1,2,128,4096]{3,2,1,0:T(8,128)(2,1)S(1)}, bf16[2,128,4096]{2,1,0:T(8,128)(2,1)S(1)}) custom-call(s32[1,2]{1,0:T(1,128)} %ids_ref.1, s32[1,1]{1,0:T(1,128)S(6)} %copy.9.count_ref, bf16[1,2,128,4096]{3,2,1,0:T(8,128)(2,1)} %deltas_ref.1, ...), custom_call_target="tpu_custom_call" | custom-call | flops 1000000000 | bytes 13000000 | tf_op jit(solution)/shard_map/pallas_call | solution.py:282
  101.0 2.3 %shard_map.86 = (f32[28,128,128]{2,1,0:T(8,128)}, bf16[28,128,128]{2,1,0:T(8,128)(2,1)}, bf16[1,2,128,4096]{3,2,1,0:T(8,128)(2,1)}) custom-call(s32[1,1]{1,0:T(1,128)S(6)} %copy.9.count_ref, f32[28,128,128]{2,1,0:T(8,128)S(1)} %get-tuple-element.10.params, bf16[28,128,128]{2,1,0:T(8,128)(2,1)S(1)} %get-tuple-element.11.momentum, ...), custom_call_target="tpu_custom_call" | custom-call | tf_op jit(solution)/shard_map/pallas_call | solution.py:314
